TPU v7x, 128 devices: a whole 4x4x4 slice. The times are simulated.
128 devices in a mesh: table: 32 (over z, x, core), sub: 4 (over y).
Axes of the slice: x: 4, y: 4, z: 4, core: 2. Of those that a mesh axis runs over, the one named last changes fastest.
Arguments:
- pooled: bfloat16 [96, 32, 4, 32, 128], P('table', None, 'sub'), may hold values from -6 to 6
- field_owner: int32 [48], replicated, may hold values from 0 to 31, as said below
- w_squeeze: float32 [16, 48], replicated, may hold values from -2.5 to 2.5
- w_excite: float32 [1536, 16], replicated, may hold values from -1.5 to 1.5
- w_bilinear: float32 [32, 32], replicated, may hold values from -1 to 1
- tower_weight: bfloat16 [36096, 1024], P(('table', 'sub')), may hold values from -0.1875 to 0.1875
- tower_cotangent: bfloat16 [1024, 16384], P(None, ('table', 'sub')), may hold values from -6 to 6
Outputs:
- row_grads: bfloat16 [96, 32, 4, 32, 128], P('table', None, 'sub')
- tower_weight_grad: float32 [36096, 1024], P(('table', 'sub'))
- squeeze_grad: float32 [16, 48], replicated
- excite_grad: float32 [1536, 16], replicated
- bilinear_grad: float32 [32, 32], replicated
Inputs may be any that keep to these rules, and one draw needn't show every extreme that they name: `field_owner`: each table index holds at most 3 fields, and some index holds exactly 3.
All inputs are finite; a program needn't handle non-finite values.
Results may differ from a plain program's by a relative error of at most 0.0074.
Values may be sent and summed in bfloat16 or wider, within the bound.
No kernel may reach another device: no remote copies, remote signals or barrier semaphores. Data moves between devices by JAX's collectives and lax.ppermute only.
A program may use at most 192 MiB of HBM per device.

v0:
```python
import jax
import jax.numpy as jnp
from jax import lax
from jax.sharding import PartitionSpec as P


def split_up(value, dim, devices):
    shape = value.shape
    blocks = value.reshape(*shape[:dim], devices, shape[dim] // devices, *shape[dim + 1 :])
    return jnp.moveaxis(blocks, dim, 0)


def piece_ends(length, count):
    turn = length // count
    if turn >= 8:
        turn -= turn % 8
    return [turn * k for k in range(1, count)]


def in_order(blocks, dim):
    shape = list(blocks.shape[1:])
    shape[dim] *= blocks.shape[0]
    return jnp.moveaxis(blocks, 0, dim).reshape(shape)


def exchange_in_pieces(value, axis, pieces, split_dim, concat_dim):
    blocks = split_up(value, split_dim, lax.axis_size(axis))
    widest = max(range(1, max(2, blocks.ndim - 1)), key=lambda d: blocks.shape[d])
    finished = []
    for share in jnp.split(blocks, piece_ends(blocks.shape[widest], pieces), axis=widest):
        if share.size:
            finished.append(lax.all_to_all(share, axis, split_axis=0, concat_axis=0, tiled=True))
    return in_order(jnp.concatenate(finished, axis=widest), concat_dim)


def from_everyone(value, axis):
    devices = lax.axis_size(axis)
    return lax.all_to_all(
        jnp.broadcast_to(value[None], (devices, *value.shape)), axis, 0, 0, tiled=True
    )


def collect(value, axis, dim):
    return in_order(from_everyone(value, axis), dim)


def hadamard_table(width):
    index = jnp.arange(width, dtype=jnp.int32)
    both = index[:, None] & index[None, :]
    parity = jnp.zeros((width, width), jnp.int32)
    for bit_pos in range(width.bit_length()):
        parity = parity ^ both >> bit_pos & 1
    return (1 - 2 * parity).astype(jnp.bfloat16)


def slot_table(field_owner, per_owner):
    count = field_owner.shape[0]
    order = jnp.arange(count, dtype=jnp.int32)
    same = field_owner[:, None] == field_owner[None, :]
    earlier = order[:, None] > order[None, :]
    position = jnp.sum((same & earlier).astype(jnp.int32), axis=1)
    return field_owner * per_owner + position


def forward(fields, w_squeeze, w_excite, w_bilinear):
    count, width, samples = fields.shape
    high = lax.Precision.HIGHEST
    squeezed = jnp.mean(fields, axis=1)
    activated = jax.nn.silu(jnp.dot(w_squeeze, squeezed, precision=high))
    excite = jnp.dot(w_excite, activated, precision=high).reshape(count, width, samples)
    weighted = fields * (1.0 + excite)
    mapped = jnp.einsum("ed,fen->fdn", w_bilinear, weighted, precision=high)
    pieces = [mapped[left][None] * weighted[left + 1 :] for left in range(count - 1)]
    pairs = jnp.concatenate(pieces, axis=0)
    return pairs.reshape(-1, samples).astype(jnp.bfloat16)


def tower_step(pair_cols, weights, piece):
    total = lax.dot_general(
        pair_cols, piece, (((1,), (1,)), ((), ())), preferred_element_type=jnp.float32
    )
    block = jnp.dot(weights, piece, preferred_element_type=jnp.float32).astype(jnp.bfloat16)
    return (total, block)


def on_device(pooled, field_owner, w_squeeze, w_excite, w_bilinear, tower_weight, tower_cotangent):
    per_owner = pooled.shape[0]
    width = pooled.shape[3]
    samples = pooled.shape[4]
    tables = lax.axis_size("table")
    total_samples = tables * lax.axis_size("sub") * samples
    scale = 1.0 / width**0.5
    signs = hadamard_table(width)
    rotated = (
        jnp.einsum("ij,ktsjb->ktsib", signs, pooled, preferred_element_type=jnp.float32) * scale
    ).astype(jnp.bfloat16)
    received = lax.all_to_all(rotated, "table", split_axis=1, concat_axis=0, tiled=True)
    received = received.reshape(per_owner * tables, width, samples)
    slot_index = slot_table(field_owner, per_owner)
    selected = jnp.take(received, slot_index, axis=0)
    fields = jnp.einsum("ij,fjn->fin", signs, selected, preferred_element_type=jnp.float32) * scale
    pairs, back = jax.vjp(forward, fields, w_squeeze, w_excite, w_bilinear)
    pair_cols = exchange_in_pieces(pairs, "table", 2, 0, 1)
    weights = collect(tower_weight, "sub", 0)
    partial_total, grads = tower_step(
        pair_cols, weights, lax.all_gather(tower_cotangent, "table", axis=1, tiled=True)
    )
    weight_total = lax.psum_scatter(partial_total, "sub", scatter_dimension=0, tiled=True)
    pair_grad = exchange_in_pieces(grads, "table", 2, 1, 0)
    field_grad, d_squeeze, d_excite, d_bilinear = back(pair_grad)
    g_squeeze, g_excite, g_bilinear = lax.psum((d_squeeze, d_excite, d_bilinear), ("table", "sub"))
    slot_count = per_owner * tables
    onehot = (slot_index[None, :] == jnp.arange(slot_count, dtype=jnp.int32)[:, None]).astype(
        jnp.bfloat16
    )
    placed = jnp.einsum(
        "sf,fen->sen", onehot, field_grad.astype(jnp.bfloat16), preferred_element_type=jnp.float32
    ).astype(jnp.bfloat16)
    placed = placed.reshape(slot_count, 1, 1, width, samples)
    row_grads = lax.all_to_all(placed, "table", split_axis=0, concat_axis=1, tiled=True)
    inverse = 1.0 / total_samples
    return (
        row_grads,
        weight_total * inverse,
        g_squeeze * inverse,
        g_excite * inverse,
        g_bilinear * inverse,
    )


def solution(mesh):
    return jax.shard_map(
        on_device,
        mesh=mesh,
        in_specs=(
            P("table", None, "sub", None, None),
            P(),
            P(),
            P(),
            P(),
            P(("table", "sub"), None),
            P(None, ("table", "sub")),
        ),
        out_specs=(P("table", None, "sub", None, None), P(("table", "sub"), None), P(), P(), P()),
        check_vma=False,
    )
```

profile of v0, /device:TPU:10, one launch (start us, length us, event | category | flops | bytes accessed | tf_op | source)
XLA Modules:
  0.0 587.5 jit_solution(3611829356810471070)
XLA Ops:
  7.9 2.8 broadcast_in_dim.19
  10.7 4.9 all-to-all-start.1
  16.9 26.4 %all-to-all-done.1 = bf16[4,282,1024]{2,1,0:T(8,128)(2,1)S(1)} async-done(((bf16[4,282,1024]{2,1,0:T(8,128)(2,1)}), bf16[4,282,1024]{2,1,0:T(8,128)(2,1)S(1)}, u32[]{:S(2)}, u32[]{:S(2)}) %all-to-all-start.1) | async-done | bytes 2310176 | tf_op jit(solution)/shard_map/all_to_all | solution.py:38
  43.3 8.5 %all-to-all-start = ((bf16[3,32,1,32,128]{4,3,0,2,1:T(8,128)(2,1)}), bf16[3,32,1,32,128]{4,3,0,2,1:T(8,128)(2,1)S(1)}, u32[]{:S(2)}, u32[]{:S(2)}) async-start(bf16[3,32,1,32,128]{4,3,0,2,1:T(8,128)(2,1)} %copy.34), calls=%async_computation | async-start | bytes 1572864 | tf_op jit(solution)/shard_map/all_to_all | solution.py:97
  51.7 2.0 reshape.337
  53.7 24.8 %all-gather.2.cloned.1.call-done = bf16[1024,4096]{1,0:T(8,128)(2,1)} async-done(((bf16[1024,128]{1,0:T(8,128)(2,1)}), bf16[1024,4096]{1,0:T(8,128)(2,1)}) %all-gather.2.cloned.1.call-update) | async-done | bytes 8388624 | tf_op jit(solution)/shard_map/all_gather | solution.py:106
  78.6 15.0 %fusion.1 = bf16[141,32,8,128]{3,2,1,0:T(8,128)(2,1)} fusion(bf16[1128,1024]{1,0:T(8,128)(2,1)} %reshape.337, bf16[1024,4096]{1,0:T(8,128)(2,1)} %all-gather.2.cloned.1.call-done), kind=kOutput, calls=%fused_computation.6 | convolution fusion | flops 9466970112 | bytes 19939328 | tf_op jit(solution)/shard_map/dot_general | solution.py:82
  93.5 8.8 %copy.49 = bf16[141,32,8,128]{3,2,0,1:T(8,128)(2,1)} copy(bf16[141,32,8,128]{3,2,1,0:T(8,128)(2,1)} %fusion.1) | data formatting | bytes 18481152 | tf_op jit(solution)/shard_map/reshape | solution.py:9
  102.3 4.7 split.345
  107.0 6.5 %all-to-all-start.2 = ((bf16[32,560,128]{2,1,0:T(8,128)(2,1)}), bf16[32,560,128]{2,1,0:T(8,128)(2,1)}, u32[]{:S(2)}, u32[]{:S(2)}) async-start(bf16[32,560,128]{2,1,0:T(8,128)(2,1)} %split.345), calls=%async_computation.2 | async-start | bytes 9175040 | tf_op jit(solution)/shard_map/all_to_all | solution.py:32
  113.6 4.9 split.346
  118.5 50.8 %all-to-all-done.2 = bf16[32,560,128]{2,1,0:T(8,128)(2,1)} async-done(((bf16[32,560,128]{2,1,0:T(8,128)(2,1)}), bf16[32,560,128]{2,1,0:T(8,128)(2,1)}, u32[]{:S(2)}, u32[]{:S(2)}) %all-to-all-start.2) | async-done | bytes 4587552 | tf_op jit(solution)/shard_map/all_to_all | solution.py:32
  169.3 7.8 %all-to-all-start.3 = ((bf16[32,568,128]{2,1,0:T(8,128)(2,1)}), bf16[32,568,128]{2,1,0:T(8,128)(2,1)}, u32[]{:S(2)}, u32[]{:S(2)}) async-start(bf16[32,568,128]{2,1,0:T(8,128)(2,1)} %split.346), calls=%async_computation.3 | async-start | bytes 9306112 | tf_op jit(solution)/shard_map/all_to_all | solution.py:32
  184.9 48.6 %all-to-all-done.3 = bf16[32,568,128]{2,1,0:T(8,128)(2,1)} async-done(((bf16[32,568,128]{2,1,0:T(8,128)(2,1)}), bf16[32,568,128]{2,1,0:T(8,128)(2,1)}, u32[]{:S(2)}, u32[]{:S(2)}) %all-to-all-start.3) | async-done | bytes 4653088 | tf_op jit(solution)/shard_map/all_to_all | solution.py:32
  233.5 4.4 pad_maximum_fusion
  241.3 1.3 multiply_reduce_fusion.45
  242.6 1.4 broadcast_multiply_fusion.44
  244.0 1.4 multiply_reduce_fusion.43
  250.7 1.4 multiply_reduce_fusion.21
  252.7 1.4 multiply_reduce_fusion.22
  254.2 1.4 multiply_reduce_fusion.23
  255.7 1.4 multiply_reduce_fusion.24
  257.2 1.4 multiply_reduce_fusion.25
  258.7 1.4 multiply_reduce_fusion.26
  260.1 1.4 multiply_reduce_fusion.27
  261.6 1.4 multiply_reduce_fusion.28
  263.0 1.4 multiply_reduce_fusion.29
  264.4 1.4 multiply_reduce_fusion.30
  265.9 1.3 multiply_reduce_fusion.32
  281.4 3.6 copy-done.3
  284.9 2.4 split.394
  287.3 7.3 %all-to-all-start.5 = ((bf16[32,560,128]{2,1,0:T(8,128)(2,1)}), bf16[32,560,128]{2,1,0:T(8,128)(2,1)}, u32[]{:S(2)}, u32[]{:S(2)}) async-start(bf16[32,560,128]{2,1,0:T(8,128)(2,1)} %split.394), calls=%async_computation.5 | async-start | bytes 9175040 | tf_op jit(solution)/shard_map/all_to_all | solution.py:32
  294.8 3.5 copy-done.4
  298.3 2.4 split.395
  301.4 1.4 multiply_reduce_fusion.20
  302.8 1.4 multiply_reduce_fusion.19
  304.3 1.5 multiply_reduce_fusion.17
  305.7 1.4 multiply_reduce_fusion.16
  307.2 1.5 multiply_reduce_fusion.14
  308.7 1.5 multiply_reduce_fusion.13
  310.2 1.5 multiply_reduce_fusion.12
  311.7 1.5 multiply_reduce_fusion.11
  313.2 1.5 multiply_reduce_fusion.10
  314.7 1.5 multiply_reduce_fusion.9
  316.3 1.5 multiply_reduce_fusion.8
  317.8 1.5 multiply_reduce_fusion.7
  319.3 1.5 multiply_reduce_fusion.6
  320.9 1.6 multiply_reduce_fusion.5
  322.4 1.6 multiply_reduce_fusion.4
  324.1 1.6 multiply_reduce_fusion.3
  325.7 24.8 %all-to-all-done.5 = bf16[32,560,128]{2,1,0:T(8,128)(2,1)} async-done(((bf16[32,560,128]{2,1,0:T(8,128)(2,1)}), bf16[32,560,128]{2,1,0:T(8,128)(2,1)}, u32[]{:S(2)}, u32[]{:S(2)}) %all-to-all-start.5) | async-done | bytes 4587552 | tf_op jit(solution)/shard_map/all_to_all | solution.py:32
  350.5 7.4 %all-to-all-start.6 = ((bf16[32,568,128]{2,1,0:T(8,128)(2,1)}), bf16[32,568,128]{2,1,0:T(8,128)(2,1)}, u32[]{:S(2)}, u32[]{:S(2)}) async-start(bf16[32,568,128]{2,1,0:T(8,128)(2,1)} %split.395), calls=%async_computation.6 | async-start | bytes 9306112 | tf_op jit(solution)/shard_map/all_to_all | solution.py:32
  361.6 13.9 %fusion.88 = (f32[48,32,128]{2,1,0:T(8,128)S(1)}, f32[48,32,128]{2,1,0:T(8,128)S(1)}) fusion(f32[48,32,128]{2,1,0:T(8,128)} %copy-done.8, f32[32,32]{1,0:T(8,128)} %param.11, f32[1,32,128]{2,1,0:T(8,128)S(1)} %bitcast.409, f32[1,32,128]{2,1,0:T(8,128)S(1)} %bitcast.407, f32[1,32,128]{2,1,0:T(8,128)S(1)} %bitcast.405, f32[1,32,128]{2,1,0:T(8,128)S(1)} %bitcast.402, ...), kind=kOutput, calls=%fused_computation.315 | convolution fusion | flops 93978624 | bytes 21614592 | tf_op jit(solution)/shard_map/transpose(jvp(ed,fen->fdn))/dot_general | solution.py:72
  375.6 1.4 fusion.67
  381.2 1.9 convolution_bitcast_fusion.2
  383.1 86.0 %all-reduce.96 = (f32[16,48]{1,0:T(8,128)S(1)}, f32[32,32]{1,0:T(8,128)S(1)}) all-reduce(f32[16,48]{1,0:T(8,128)S(1)} %fusion.54, f32[32,32]{1,0:T(8,128)S(1)} %convolution_bitcast_fusion.2), channel_id=1, replica_groups=mesh['table'=32,'sub'=4] {'table','sub'}, use_global_device_ids=true, to_apply=%region_49.50 | all-reduce | flops 1792 | bytes 14336 | tf_op jit(solution)/shard_map/psum | solution.py:111
  470.4 6.4 %all-to-all-start.4 = ((bf16[96,1,1,32,128]{4,3,2,1,0:T(8,128)(2,1)}), bf16[96,1,1,32,128]{4,3,2,1,0:T(8,128)(2,1)S(1)}, u32[]{:S(2)}, u32[]{:S(2)}) async-start(bf16[96,1,1,32,128]{4,3,2,1,0:T(8,128)(2,1)} %copy.39), calls=%async_computation.4 | async-start | bytes 1572864 | tf_op jit(solution)/shard_map/all_to_all | solution.py:120
  476.8 7.4 %maximum_bitcast_fusion = bf16[1128,32,128]{2,0,1:T(8,128)(2,1)} fusion(bf16[32,568,128]{2,1,0:T(8,128)(2,1)} %all-to-all-done.6, bf16[32,560,128]{2,1,0:T(8,128)(2,1)} %all-to-all-done.5), kind=kLoop, calls=%fused_computation.4 | loop fusion | flops 18481152 | bytes 18481152 | tf_op jit(solution)/shard_map/transpose | solution.py:23
  484.2 12.6 %copy.40 = bf16[1128,32,128]{0,2,1:T(8,128)(2,1)} copy(bf16[1128,32,128]{2,0,1:T(8,128)(2,1)} %maximum_bitcast_fusion) | data formatting | bytes 18481152 | tf_op jit(solution)/shard_map/transpose | solution.py:23
  496.8 16.0 %fusion.89 = f32[1128,1024]{1,0:T(8,128)} fusion(bf16[1128,4096]{0,1:T(8,128)(2,1)} %bitcast.343, bf16[1024,4096]{1,0:T(8,128)(2,1)} %all-gather.2.cloned.1.call-done), kind=kOutput, calls=%fused_computation.316 | convolution fusion | flops 9462349824 | bytes 22249472 | tf_op jit(solution)/shard_map/dot_general | solution.py:79
  512.8 58.7 %fusion = f32[288,1024]{1,0:T(8,128)S(1)} fusion(f32[1128,1024]{1,0:T(8,128)} %fusion.89), kind=kCustom, calls=%all-reduce-scatter | all-reduce-scatter fusion | flops 1179649 | bytes 5800448
  571.5 2.3 collective-permute-start
  573.8 1.5 broadcast_multiply_fusion.41
  576.3 1.7 collective-permute-done
  (373 shorter events, 45.0 us)
Async XLA Ops:
  7.2 71.4 %all-gather.2.cloned.1.call-start = ((), (), s32[]{:S(2)}) async-start(), calls=%async_computation.7 | async-start | bytes 8650752 | tf_op jit(solution)/shard_map/all_gather | solution.py:106
  10.7 32.6 %all-to-all-start.1 = ((bf16[4,282,1024]{2,1,0:T(8,128)(2,1)}), bf16[4,282,1024]{2,1,0:T(8,128)(2,1)S(1)}, u32[]{:S(2)}, u32[]{:S(2)}) async-start(bf16[4,282,1024]{2,1,0:T(8,128)(2,1)} %broadcast_in_dim.19), calls=%async_computation.1 | async-start | bytes 4718592 | tf_op jit(solution)/shard_map/all_to_all | solution.py:38
  43.3 63.8 %all-to-all-start = ((bf16[3,32,1,32,128]{4,3,0,2,1:T(8,128)(2,1)}), bf16[3,32,1,32,128]{4,3,0,2,1:T(8,128)(2,1)S(1)}, u32[]{:S(2)}, u32[]{:S(2)}) async-start(bf16[3,32,1,32,128]{4,3,0,2,1:T(8,128)(2,1)} %copy.34), calls=%async_computation | async-start | bytes 1572864 | tf_op jit(solution)/shard_map/all_to_all | solution.py:97
  107.0 62.2 %all-to-all-start.2 = ((bf16[32,560,128]{2,1,0:T(8,128)(2,1)}), bf16[32,560,128]{2,1,0:T(8,128)(2,1)}, u32[]{:S(2)}, u32[]{:S(2)}) async-start(bf16[32,560,128]{2,1,0:T(8,128)(2,1)} %split.345), calls=%async_computation.2 | async-start | bytes 9175040 | tf_op jit(solution)/shard_map/all_to_all | solution.py:32
  113.5 63.5 %copy-start.89 = (u32[128]{0:T(128)S(1)}, u32[128]{0:T(128)}, u32[]{:S(2)}) copy-start(u32[128]{0:T(128)} %constant.239) | copy-start | bytes 1540
  113.5 64.7 %copy-start.90 = (s32[48]{0:T(128)S(1)}, s32[48]{0:T(128)}, u32[]{:S(2)}) copy-start(s32[48]{0:T(128)} %param.8) | copy-start | bytes 580
  113.6 66.5 %copy-start.87 = (f32[16,48]{1,0:T(8,128)S(1)}, f32[16,48]{1,0:T(8,128)}, u32[]{:S(2)}) copy-start(f32[16,48]{1,0:T(8,128)} %param.9) | copy-start | bytes 9220
  113.6 67.6 %copy-start.10 = (f32[1536,16]{0,1:T(8,128)S(1)}, f32[1536,16]{0,1:T(8,128)}, u32[]{:S(2)}) copy-start(f32[1536,16]{0,1:T(8,128)} %param.10) | copy-start | bytes 294916
  118.5 64.0 %copy-start.78 = (f32[32,32]{1,0:T(8,128)S(1)}, f32[32,32]{1,0:T(8,128)}, u32[]{:S(2)}) copy-start(f32[32,32]{1,0:T(8,128)} %param.11) | copy-start | bytes 12292
  169.3 64.2 %all-to-all-start.3 = ((bf16[32,568,128]{2,1,0:T(8,128)(2,1)}), bf16[32,568,128]{2,1,0:T(8,128)(2,1)}, u32[]{:S(2)}, u32[]{:S(2)}) async-start(bf16[32,568,128]{2,1,0:T(8,128)(2,1)} %split.346), calls=%async_computation.3 | async-start | bytes 9306112 | tf_op jit(solution)/shard_map/all_to_all | solution.py:32
  182.3 55.6 %copy-start.5 = (f32[1536,128]{1,0:T(8,128)}, f32[1536,128]{1,0:T(8,128)S(1)}, u32[]{:S(2)}) copy-start(f32[1536,128]{1,0:T(8,128)S(1)} %copy.35) | copy-start | bytes 2359300
  183.3 55.9 %copy-start.7 = (f32[48,32,128]{2,1,0:T(8,128)}, f32[48,32,128]{2,1,0:T(8,128)S(1)}, u32[]{:S(2)}) copy-start(f32[48,32,128]{2,1,0:T(8,128)S(1)} %convolution_bitcast_fusion.1) | copy-start | bytes 2359300
  184.1 58.5 %copy-start.51 = (f32[32,128]{1,0:T(8,128)}, f32[32,128]{1,0:T(8,128)S(1)}, u32[]{:S(2)}) copy-start(f32[32,128]{1,0:T(8,128)S(1)} %get-tuple-element.71) | copy-start | bytes 49156
  184.1 61.4 %copy-start.66 = (f32[32,128]{1,0:T(8,128)}, f32[32,128]{1,0:T(8,128)S(1)}, u32[]{:S(2)}) copy-start(f32[32,128]{1,0:T(8,128)S(1)} %get-tuple-element.67) | copy-start | bytes 49156
  184.8 55.3 %copy-start.64 = (f32[32,128]{1,0:T(8,128)}, f32[32,128]{1,0:T(8,128)S(1)}, u32[]{:S(2)}) copy-start(f32[32,128]{1,0:T(8,128)S(1)} %get-tuple-element.41) | copy-start | bytes 49156
  184.8 61.9 %copy-start.61 = (f32[32,128]{1,0:T(8,128)}, f32[32,128]{1,0:T(8,128)S(1)}, u32[]{:S(2)}) copy-start(f32[32,128]{1,0:T(8,128)S(1)} %get-tuple-element.58) | copy-start | bytes 49156
  184.8 63.3 %copy-start.49 = (f32[32,128]{1,0:T(8,128)}, f32[32,128]{1,0:T(8,128)S(1)}, u32[]{:S(2)}) copy-start(f32[32,128]{1,0:T(8,128)S(1)} %get-tuple-element.42) | copy-start | bytes 49156
  184.8 67.3 %copy-start.29 = (f32[32,128]{1,0:T(8,128)}, f32[32,128]{1,0:T(8,128)S(1)}, u32[]{:S(2)}) copy-start(f32[32,128]{1,0:T(8,128)S(1)} %get-tuple-element.43) | copy-start | bytes 49156
  184.8 67.4 %copy-start.31 = (f32[32,128]{1,0:T(8,128)}, f32[32,128]{1,0:T(8,128)S(1)}, u32[]{:S(2)}) copy-start(f32[32,128]{1,0:T(8,128)S(1)} %get-tuple-element.44) | copy-start | bytes 49156
  184.8 67.5 %copy-start.28 = (f32[32,128]{1,0:T(8,128)}, f32[32,128]{1,0:T(8,128)S(1)}, u32[]{:S(2)}) copy-start(f32[32,128]{1,0:T(8,128)S(1)} %get-tuple-element.45) | copy-start | bytes 49156
  252.5 16.1 %slice-start.8 = ((f32[36096,128]{1,0:T(8,128)}), f32[416,128]{1,0:T(8,128)S(1)}, s32[]{:S(2)}) async-start(f32[36096,128]{1,0:T(8,128)} %copy-done.2), calls=%async_computation.17 | async-start | bytes 425984 | tf_op jit(solution)/shard_map/transpose(jvp())/split | solution.py:74
  252.6 17.4 %slice-start.7 = ((f32[36096,128]{1,0:T(8,128)}), f32[384,128]{1,0:T(8,128)S(1)}, s32[]{:S(2)}) async-start(f32[36096,128]{1,0:T(8,128)} %copy-done.2), calls=%async_computation.16 | async-start | bytes 393216 | tf_op jit(solution)/shard_map/transpose(jvp())/split | solution.py:74
  252.6 17.4 %copy-start.58 = (f32[32,128]{1,0:T(8,128)S(1)}, f32[32,128]{1,0:T(8,128)}, u32[]{:S(2)}) copy-start(f32[32,128]{1,0:T(8,128)} %get-tuple-element.63) | copy-start | bytes 49156
  252.7 18.7 %slice-start.6 = ((f32[36096,128]{1,0:T(8,128)}), f32[352,128]{1,0:T(8,128)S(1)}, s32[]{:S(2)}) async-start(f32[36096,128]{1,0:T(8,128)} %copy-done.2), calls=%async_computation.15 | async-start | bytes 360448 | tf_op jit(solution)/shard_map/transpose(jvp())/split | solution.py:74
  252.7 18.7 %copy-start.57 = (f32[32,128]{1,0:T(8,128)S(1)}, f32[32,128]{1,0:T(8,128)}, u32[]{:S(2)}) copy-start(f32[32,128]{1,0:T(8,128)} %get-tuple-element.64) | copy-start | bytes 49156
  254.1 18.6 %slice-start.5 = ((f32[36096,128]{1,0:T(8,128)}), f32[320,128]{1,0:T(8,128)S(1)}, s32[]{:S(2)}) async-start(f32[36096,128]{1,0:T(8,128)} %copy-done.2), calls=%async_computation.14 | async-start | bytes 327680 | tf_op jit(solution)/shard_map/transpose(jvp())/split | solution.py:74
  254.1 18.6 %copy-start.56 = (f32[32,128]{1,0:T(8,128)S(1)}, f32[32,128]{1,0:T(8,128)}, u32[]{:S(2)}) copy-start(f32[32,128]{1,0:T(8,128)} %get-tuple-element.65) | copy-start | bytes 49156
  254.2 19.8 %slice-start.4 = ((f32[36096,128]{1,0:T(8,128)}), f32[288,128]{1,0:T(8,128)S(1)}, s32[]{:S(2)}) async-start(f32[36096,128]{1,0:T(8,128)} %copy-done.2), calls=%async_computation.13 | async-start | bytes 294912 | tf_op jit(solution)/shard_map/transpose(jvp())/split | solution.py:74
  255.6 19.8 %copy-start.67 = (f32[32,128]{1,0:T(8,128)S(1)}, f32[32,128]{1,0:T(8,128)}, u32[]{:S(2)}) copy-start(f32[32,128]{1,0:T(8,128)} %copy-done.66) | copy-start | bytes 49156
  255.6 19.8 %slice-start.3 = ((f32[36096,128]{1,0:T(8,128)}), f32[224,128]{1,0:T(8,128)S(1)}, s32[]{:S(2)}) async-start(f32[36096,128]{1,0:T(8,128)} %copy-done.2), calls=%async_computation.12 | async-start | bytes 229376 | tf_op jit(solution)/shard_map/transpose(jvp())/split | solution.py:74
  255.6 19.8 %copy-start.55 = (f32[32,128]{1,0:T(8,128)S(1)}, f32[32,128]{1,0:T(8,128)}, u32[]{:S(2)}) copy-start(f32[32,128]{1,0:T(8,128)} %get-tuple-element.68) | copy-start | bytes 49156
  255.7 18.4 %copy-start.70 = (f32[32,128]{1,0:T(8,128)S(1)}, f32[32,128]{1,0:T(8,128)}, u32[]{:S(2)}) copy-start(f32[32,128]{1,0:T(8,128)} %get-tuple-element.66) | copy-start | bytes 49156
  255.7 21.0 %slice-start.2 = ((f32[36096,128]{1,0:T(8,128)}), f32[192,128]{1,0:T(8,128)S(1)}, s32[]{:S(2)}) async-start(f32[36096,128]{1,0:T(8,128)} %copy-done.2), calls=%async_computation.11 | async-start | bytes 196608 | tf_op jit(solution)/shard_map/transpose(jvp())/split | solution.py:74
  255.7 21.0 %copy-start.54 = (f32[32,128]{1,0:T(8,128)S(1)}, f32[32,128]{1,0:T(8,128)}, u32[]{:S(2)}) copy-start(f32[32,128]{1,0:T(8,128)} %get-tuple-element.69) | copy-start | bytes 49156
  255.7 22.3 %slice-start.1 = ((f32[36096,128]{1,0:T(8,128)}), f32[160,128]{1,0:T(8,128)S(1)}, s32[]{:S(2)}) async-start(f32[36096,128]{1,0:T(8,128)} %copy-done.2), calls=%async_computation.10 | async-start | bytes 163840 | tf_op jit(solution)/shard_map/transpose(jvp())/split | solution.py:74
  255.7 22.3 %copy-start.53 = (f32[32,128]{1,0:T(8,128)S(1)}, f32[32,128]{1,0:T(8,128)}, u32[]{:S(2)}) copy-start(f32[32,128]{1,0:T(8,128)} %get-tuple-element.70) | copy-start | bytes 49156
  257.2 22.1 %copy-start.52 = (f32[32,128]{1,0:T(8,128)S(1)}, f32[32,128]{1,0:T(8,128)}, u32[]{:S(2)}) copy-start(f32[32,128]{1,0:T(8,128)} %copy-done.51) | copy-start | bytes 49156
  257.2 22.2 %slice-start = ((f32[36096,128]{1,0:T(8,128)}), f32[96,128]{1,0:T(8,128)S(1)}, s32[]{:S(2)}) async-start(f32[36096,128]{1,0:T(8,128)} %copy-done.2), calls=%async_computation.9 | async-start | bytes 98304 | tf_op jit(solution)/shard_map/transpose(jvp())/split | solution.py:74
  257.2 22.2 %copy-start.68 = (f32[32,128]{1,0:T(8,128)S(1)}, f32[32,128]{1,0:T(8,128)}, u32[]{:S(2)}) copy-start(f32[32,128]{1,0:T(8,128)} %get-tuple-element.60) | copy-start | bytes 49156
  257.2 23.4 %copy-start.65 = (f32[32,128]{1,0:T(8,128)S(1)}, f32[32,128]{1,0:T(8,128)}, u32[]{:S(2)}) copy-start(f32[32,128]{1,0:T(8,128)} %copy-done.64) | copy-start | bytes 49156
  287.3 63.2 %all-to-all-start.5 = ((bf16[32,560,128]{2,1,0:T(8,128)(2,1)}), bf16[32,560,128]{2,1,0:T(8,128)(2,1)}, u32[]{:S(2)}, u32[]{:S(2)}) async-start(bf16[32,560,128]{2,1,0:T(8,128)(2,1)} %split.394), calls=%async_computation.5 | async-start | bytes 9175040 | tf_op jit(solution)/shard_map/all_to_all | solution.py:32
  300.7 15.5 %slice-start.33 = ((f32[36096,128]{1,0:T(8,128)}), f32[1248,128]{1,0:T(8,128)S(1)}, s32[]{:S(2)}) async-start(f32[36096,128]{1,0:T(8,128)} %copy-done.2), calls=%async_computation.42 | async-start | bytes 1277952 | tf_op jit(solution)/shard_map/transpose(jvp())/split | solution.py:74
  300.7 15.5 %copy-start.23 = (f32[32,128]{1,0:T(8,128)S(1)}, f32[32,128]{1,0:T(8,128)}, u32[]{:S(2)}) copy-start(f32[32,128]{1,0:T(8,128)} %copy-done.22) | copy-start | bytes 49156
  301.4 16.4 %slice-start.34 = ((f32[36096,128]{1,0:T(8,128)}), f32[1280,128]{1,0:T(8,128)S(1)}, s32[]{:S(2)}) async-start(f32[36096,128]{1,0:T(8,128)} %copy-done.2), calls=%async_computation.43 | async-start | bytes 1310720 | tf_op jit(solution)/shard_map/transpose(jvp())/split | solution.py:74
  301.4 16.4 %copy-start.21 = (f32[32,128]{1,0:T(8,128)S(1)}, f32[32,128]{1,0:T(8,128)}, u32[]{:S(2)}) copy-start(f32[32,128]{1,0:T(8,128)} %copy-done.20) | copy-start | bytes 49156
  302.8 16.5 %slice-start.35 = ((f32[36096,128]{1,0:T(8,128)}), f32[1312,128]{1,0:T(8,128)S(1)}, s32[]{:S(2)}) async-start(f32[36096,128]{1,0:T(8,128)} %copy-done.2), calls=%async_computation.44 | async-start | bytes 1343488 | tf_op jit(solution)/shard_map/transpose(jvp())/split | solution.py:74
  308.7 15.4 %slice-start.38 = ((f32[36096,128]{1,0:T(8,128)}), f32[1408,128]{1,0:T(8,128)S(1)}, s32[]{:S(2)}) async-start(f32[36096,128]{1,0:T(8,128)} %copy-done.2), calls=%async_computation.47 | async-start | bytes 1441792 | tf_op jit(solution)/shard_map/transpose(jvp())/split | solution.py:74
  319.3 40.1 %slice-start.24 = ((f32[36096,128]{1,0:T(8,128)}), f32[928,128]{1,0:T(8,128)S(1)}, s32[]{:S(2)}) async-start(f32[36096,128]{1,0:T(8,128)} %copy-done.2), calls=%async_computation.33 | async-start | bytes 950272 | tf_op jit(solution)/shard_map/transpose(jvp())/split | solution.py:74
  322.4 37.8 %slice-start.39 = ((f32[36096,128]{1,0:T(8,128)}), f32[1440,128]{1,0:T(8,128)S(1)}, s32[]{:S(2)}) async-start(f32[36096,128]{1,0:T(8,128)} %copy-done.2), calls=%async_computation.48 | async-start | bytes 1474560 | tf_op jit(solution)/shard_map/transpose(jvp())/split | solution.py:74
  324.1 37.1 %slice-start.40 = ((f32[36096,128]{1,0:T(8,128)}), f32[1472,128]{1,0:T(8,128)S(1)}, s32[]{:S(2)}) async-start(f32[36096,128]{1,0:T(8,128)} %copy-done.2), calls=%async_computation.49 | async-start | bytes 1507328 | tf_op jit(solution)/shard_map/transpose(jvp())/split | solution.py:74
  324.1 37.1 %copy-start.18 = (f32[32,128]{1,0:T(8,128)S(1)}, f32[32,128]{1,0:T(8,128)}, u32[]{:S(2)}) copy-start(f32[32,128]{1,0:T(8,128)} %copy-done.17) | copy-start | bytes 49156
  324.1 37.3 %copy-start.16 = (f32[32,128]{1,0:T(8,128)S(1)}, f32[32,128]{1,0:T(8,128)}, u32[]{:S(2)}) copy-start(f32[32,128]{1,0:T(8,128)} %copy-done.15) | copy-start | bytes 49156
  325.7 35.8 %copy-start.12 = (f32[14,32,128]{2,1,0:T(8,128)S(1)}, f32[14,32,128]{2,1,0:T(8,128)}, u32[]{:S(2)}) copy-start(f32[14,32,128]{2,1,0:T(8,128)} %get-tuple-element.135) | copy-start | bytes 688132
  350.5 119.9 %all-to-all-start.6 = ((bf16[32,568,128]{2,1,0:T(8,128)(2,1)}), bf16[32,568,128]{2,1,0:T(8,128)(2,1)}, u32[]{:S(2)}, u32[]{:S(2)}) async-start(bf16[32,568,128]{2,1,0:T(8,128)(2,1)} %split.395), calls=%async_computation.6 | async-start | bytes 9306112 | tf_op jit(solution)/shard_map/all_to_all | solution.py:32
  357.9 215.9 %all-reduce.99.cloned.1.call-start = ((), (), s32[]{:S(2)}) async-start(), calls=%async_computation.8 | async-start | bytes 196608 | tf_op jit(solution)/shard_map/psum | solution.py:111
  361.6 15.5 %copy-start.11 = (f32[1536,16]{0,1:T(8,128)S(1)}, f32[1536,16]{0,1:T(8,128)}, u32[]{:S(2)}) copy-start(f32[1536,16]{0,1:T(8,128)} %param.10) | copy-start | bytes 294916
  361.6 16.9 %copy-start.6 = (f32[1536,128]{1,0:T(8,128)S(1)}, f32[1536,128]{1,0:T(8,128)}, u32[]{:S(2)}) copy-start(f32[1536,128]{1,0:T(8,128)} %copy-done.5) | copy-start | bytes 2359300
  361.6 19.4 %copy-start.14 = (f32[48,128]{1,0:T(8,128)S(1)}, f32[48,128]{1,0:T(8,128)}, u32[]{:S(2)}) copy-start(f32[48,128]{1,0:T(8,128)} %copy-done.13) | copy-start | bytes 73732
  361.6 19.5 %copy-start.79 = (f32[32,128]{1,0:T(8,128)S(1)}, f32[32,128]{1,0:T(8,128)}, u32[]{:S(2)}) copy-start(f32[32,128]{1,0:T(8,128)} %multiply_reduce_fusion.15) | copy-start | bytes 49156
  361.6 19.6 %copy-start.80 = (f32[32,128]{1,0:T(8,128)S(1)}, f32[32,128]{1,0:T(8,128)}, u32[]{:S(2)}) copy-start(f32[32,128]{1,0:T(8,128)} %get-tuple-element.112) | copy-start | bytes 49156
  361.6 19.6 %copy-start.81 = (f32[32,128]{1,0:T(8,128)S(1)}, f32[32,128]{1,0:T(8,128)}, u32[]{:S(2)}) copy-start(f32[32,128]{1,0:T(8,128)} %get-tuple-element.114) | copy-start | bytes 49156
  470.4 105.0 %all-to-all-start.4 = ((bf16[96,1,1,32,128]{4,3,2,1,0:T(8,128)(2,1)}), bf16[96,1,1,32,128]{4,3,2,1,0:T(8,128)(2,1)S(1)}, u32[]{:S(2)}, u32[]{:S(2)}) async-start(bf16[96,1,1,32,128]{4,3,2,1,0:T(8,128)(2,1)} %copy.39), calls=%async_computation.4 | async-start | bytes 1572864 | tf_op jit(solution)/shard_map/all_to_all | solution.py:120
  496.8 83.4 %copy-start.1 = (bf16[3,32,1,32,128]{4,3,2,1,0:T(8,128)(2,1)S(1)}, bf16[3,32,1,32,128]{4,3,2,1,0:T(8,128)(2,1)}, u32[]{:S(2)}) copy-start(bf16[3,32,1,32,128]{4,3,2,1,0:T(8,128)(2,1)} %param.7) | copy-start | bytes 2359300
  571.5 6.5 %collective-permute-start = (f32[18,1024]{1,0:T(8,128)S(1)}, f32[18,1024]{1,0:T(8,128)S(1)}, u32[]{:S(2)}, u32[]{:S(2)}) collective-permute-start(f32[18,1024]{1,0:T(8,128)S(1)} %slice.519), channel_id=1, source_target_pairs={{0,1},{1,2},{2,3},{4,5},{5,6},{6,7},{8,9},{9,10},{10,11},{12,13},{... | collective-permute-start | bytes 221192
  (78 other events, 733.1 us)
Sparse Core Ops, SparseCore 0:
  10.2 68.3 all-gather.1
  377.2 158.5 all-reduce.98
where the time goes:
time: 596 us; the launch traced here: 588 us
  waiting for transfers between devices  178 us (30%)
  blocking collectives  145 us (24%)
  other arithmetic  85.3 us (14%)
  local copies, waits for them, and re-layouts  58 us (10%)
  matrix products  53.3 us (9%)
  starting transfers between devices  51.3 us (9%)
  between operations  16.9 us (3%)
    all_to_all x4, waiting for transfers between devices, exchange_in_pieces(): lax.all_to_all(share, axis, split_axis=0, concat_axis=0, tiled=True)  124 us
    psum x1, blocking collectives, on_device(): lax.psum((d_squeeze, d_excite, d_bilinear), ('table', 'sub'))  86 us
    reduce_sum x46, other arithmetic, forward(): mapped[left][None] * weighted[left + 1:]  58.9 us
    unnamed x1, blocking collectives  58.7 us
    all_to_all x4, starting transfers between devices, exchange_in_pieces(): lax.all_to_all(share, axis, split_axis=0, concat_axis=0, tiled=True)  29 us
    all_to_all x1, waiting for transfers between devices, from_everyone(): lax.all_to_all(jnp.broadcast_to(value[None], (devices, *value.shape)), ax...  26.4 us
    all_gather x1, waiting for transfers between devices, on_device(): lax.all_gather(tower_cotangent, 'table', axis=1, tiled=True)  24.8 us
    dot_general x3, matrix products, forward(): mapped = jnp.einsum('ed,fen->fdn', w_bilinear, weighted, precision=high)  16.6 us
  transfers between devices with their start and end apart: 10, of which 6 were waited for; matrix products, arithmetic and copies ran while one was open for 33% of the time, Pallas kernels for 0%

commit v1 on v0

v1 whole, which is shorter than its diff:
```python
import jax
import jax.numpy as jnp
import numpy as np
from jax import lax
from jax.sharding import PartitionSpec as P

HIGH = lax.Precision.HIGHEST
BOTH = ("table", "sub")


def block_plan(tables):
    groups = int(round((2 * tables) ** 0.5))
    blocks = [(a, b) for a in range(groups) for b in range(a + 1, groups)]
    straight = len(blocks)
    blocks += [(a, a + 1) for a in range(0, groups, 2)]
    assert len(blocks) == tables
    return groups, straight, blocks


def color_edges(edges, left, right):
    degree_l = np.bincount([e[0] for e in edges], minlength=left)
    degree_r = np.bincount([e[1] for e in edges], minlength=right)
    colors = int(max(degree_l.max(), degree_r.max()))
    at_l = -np.ones((left, colors), int)
    at_r = -np.ones((right, colors), int)
    chosen = [-1] * len(edges)
    for k, (u, v) in enumerate(edges):
        a = int(np.where(at_l[u] < 0)[0][0])
        b = int(np.where(at_r[v] < 0)[0][0])
        if a != b:
            path, node, on_right, want = [], v, True, a
            while True:
                e = int((at_r if on_right else at_l)[node][want])
                if e < 0:
                    break
                path.append(e)
                node = edges[e][0] if on_right else edges[e][1]
                on_right = not on_right
                want = b if want == a else a
            for e in path:
                at_l[edges[e][0], chosen[e]] = -1
                at_r[edges[e][1], chosen[e]] = -1
            for e in path:
                chosen[e] = b if chosen[e] == a else a
                at_l[edges[e][0], chosen[e]] = e
                at_r[edges[e][1], chosen[e]] = e
        chosen[k] = a
        at_l[u, a] = k
        at_r[v, a] = k
    return colors, chosen


def row_plan(fields, tables, subs, width, rows):
    devices = tables * subs
    groups, straight, blocks = block_plan(tables)
    size = fields // groups
    share = size * size // subs
    pair_at = {}
    for i in range(fields):
        for j in range(i + 1, fields):
            pair_at[(i, j)] = len(pair_at)
    place = {}
    for r, (g, h) in enumerate(blocks):
        for a in range(size):
            for b in range(size):
                if r < straight:
                    pair = (g * size + a, h * size + b)
                elif a < b:
                    pair = (g * size + a, g * size + b)
                elif a > b:
                    pair = (h * size + b, h * size + a)
                else:
                    continue
                slot = a * size + b
                place[pair_at[pair]] = (r * subs + slot // share, slot % share)
    count = len(pair_at)
    assert len(place) == count and count * width == rows * devices
    first = [-(-rows * d // width) for d in range(devices + 1)]
    out_edges, out_info = [], []
    for g in range(count):
        d = width * g // rows
        out_edges.append((d, place[g][0]))
        out_info.append((g - first[d], place[g][1]))
    n_out, out_color = color_edges(out_edges, devices, devices)
    take = np.zeros((devices, n_out), np.int32)
    put = -np.ones((devices, share), np.int32)
    perms = [[] for _ in range(n_out)]
    used = np.zeros((devices, n_out), bool)
    for (u, v), (k, slot), c in zip(out_edges, out_info, out_color):
        perms[c].append((u, v))
        take[u, c] = width * first[u] - rows * u + width * k
        put[v, slot] = c
        used[v, c] = True
    for v in range(devices):
        for slot in range(share):
            if put[v, slot] < 0:
                put[v, slot] = int(np.where(~used[v])[0][0])
    back_edges, back_info = [], []
    low = [rows * d // width for d in range(devices)]
    span = 0
    for d in range(devices):
        for g in range(low[d], (rows * (d + 1) - 1) // width + 1):
            back_edges.append((place[g][0], d))
            back_info.append((place[g][1], g - low[d]))
            span = max(span, g - low[d] + 1)
    n_back, back_color = color_edges(back_edges, devices, devices)
    b_take = np.zeros((devices, n_back), np.int32)
    b_put = np.zeros((devices, span), np.int32)
    b_perms = [[] for _ in range(n_back)]
    for (u, v), (k, q), c in zip(back_edges, back_info, back_color):
        b_perms[c].append((u, v))
        b_take[u, c] = k
        b_put[v, q] = c
    b_off = np.array([rows * d - width * low[d] for d in range(devices)], np.int32)
    return dict(perms=perms, take=take, put=put, b_perms=b_perms, b_take=b_take, b_put=b_put, b_off=b_off)


def hadamard_table(width):
    index = jnp.arange(width, dtype=jnp.int32)
    both = index[:, None] & index[None, :]
    parity = jnp.zeros((width, width), jnp.int32)
    for bit_pos in range(width.bit_length()):
        parity = parity ^ both >> bit_pos & 1
    return (1 - 2 * parity).astype(jnp.bfloat16)


def slot_table(field_owner, per_owner):
    count = field_owner.shape[0]
    order = jnp.arange(count, dtype=jnp.int32)
    same = field_owner[:, None] == field_owner[None, :]
    earlier = order[:, None] > order[None, :]
    position = jnp.sum((same & earlier).astype(jnp.int32), axis=1)
    return field_owner * per_owner + position


def excited(fields, w_squeeze, w_excite):
    squeezed = jnp.mean(fields, axis=1)
    activated = jax.nn.silu(jnp.dot(w_squeeze, squeezed, precision=HIGH))
    excite = jnp.dot(w_excite, activated, precision=HIGH).reshape(fields.shape)
    return fields * (1.0 + excite)


def on_device(pooled, field_owner, w_squeeze, w_excite, w_bilinear, tower_weight, tower_cotangent):
    f32, bf16 = jnp.float32, jnp.bfloat16
    per_owner, _, _, width, samples = pooled.shape
    tables, subs = lax.axis_size("table"), lax.axis_size("sub")
    total_samples = tables * subs * samples
    count = field_owner.shape[0]
    rows, hidden = tower_weight.shape
    plan = row_plan(count, tables, subs, width, rows)
    groups, straight, blocks = block_plan(tables)
    size = count // groups
    scale = 1.0 / width**0.5
    signs = hadamard_table(width)
    me = lax.axis_index(BOTH)
    row_group = lax.axis_index("table")
    diag = row_group >= straight
    cols = tables * samples

    rotated = (
        jnp.einsum("ij,ktsjb->ktsib", signs, pooled, preferred_element_type=f32) * scale
    ).astype(bf16)
    received = lax.all_to_all(rotated, "table", split_axis=1, concat_axis=0, tiled=True)
    received = received.reshape(per_owner * tables, width, samples)
    slot_index = slot_table(field_owner, per_owner)
    selected = jnp.take(received, slot_index, axis=0)

    needed = np.array(blocks, np.int32).reshape(-1)
    by_group = selected.reshape(groups, size * width, samples)
    sent = jnp.concatenate([by_group[int(g)][None] for g in needed], axis=0)
    sent = sent.reshape(tables, 2 * size * width, samples)
    squeeze_rows = jnp.broadcast_to(selected[:, 0, :][None], (tables, count, samples))
    sent = jnp.concatenate([sent, squeeze_rows], axis=1)
    got = lax.all_to_all(sent, "table", split_axis=0, concat_axis=0, tiled=True)
    got = jnp.moveaxis(got, 0, 1).reshape(2 * size * width + count, cols)

    nearby = lax.ppermute(
        tower_weight[:width], BOTH, [(d + 1, d) for d in range(tables * subs - 1)]
    )
    extended = jnp.concatenate([tower_weight, nearby], axis=0)
    take = jnp.asarray(plan["take"])[me]
    arrived = []
    for c, perm in enumerate(plan["perms"]):
        piece = lax.dynamic_slice(extended, (take[c], 0), (width, hidden))
        arrived.append(lax.ppermute(piece, BOTH, perm))
    mine = jnp.take(jnp.stack(arrived), jnp.asarray(plan["put"])[me], axis=0)
    mine = mine.reshape(-1, hidden)
    weights = lax.all_to_all(
        jnp.broadcast_to(mine[None], (subs, *mine.shape)), "sub", 0, 0, tiled=True
    ).reshape(-1, hidden)

    cotangent = lax.all_gather(tower_cotangent, "table", axis=1, tiled=True)
    pair_grad = jnp.dot(weights, cotangent, preferred_element_type=f32).astype(bf16)
    pair_grad = pair_grad.reshape(size, size, width, cols)

    chosen = got[: 2 * size * width].reshape(2 * size, width, cols)
    fields = jnp.einsum("ij,fjn->fin", signs, chosen, preferred_element_type=f32) * scale
    squeezed = got[2 * size * width :].astype(f32) * scale
    activated = jax.nn.silu(jnp.dot(w_squeeze, squeezed, precision=HIGH))
    mine_groups = jnp.asarray(np.array(blocks, np.int32))[row_group]
    w_here = jnp.take(w_excite.reshape(groups, size * width, -1), mine_groups, axis=0)
    w_here = w_here.reshape(2 * size * width, -1)
    excite = jnp.dot(w_here, activated, precision=HIGH).reshape(fields.shape)
    weighted = fields * (1.0 + excite)
    mapped = jnp.einsum("ed,fen->fdn", w_bilinear, weighted, precision=HIGH)
    m1, m2, w1, w2 = mapped[:size], mapped[size:], weighted[:size], weighted[size:]
    x_up, x_lo = m1, jnp.where(diag, w2, m1)
    y_up, y_lo = jnp.where(diag, w1, w2), jnp.where(diag, m2, w2)

    pg = pair_grad.astype(f32)
    zero = jnp.zeros((width, cols), f32)
    dx_up = jnp.stack([sum((pg[a, b] * y_up[b] for b in range(a + 1, size)), zero) for a in range(size)])
    dx_lo = jnp.stack([sum((pg[a, b] * y_lo[b] for b in range(a + 1)), zero) for a in range(size)])
    dy_up = jnp.stack([sum((pg[a, b] * x_up[a] for a in range(b)), zero) for b in range(size)])
    dy_lo = jnp.stack([sum((pg[a, b] * x_lo[a] for a in range(b, size)), zero) for b in range(size)])
    dm = jnp.concatenate([dx_up + jnp.where(diag, 0.0, dx_lo), jnp.where(diag, dy_lo, 0.0)], axis=0)
    dw = jnp.concatenate(
        [jnp.where(diag, dy_up, 0.0), jnp.where(diag, dx_lo, dy_up + dy_lo)], axis=0
    )
    d_bilinear = jnp.einsum("fen,fdn->ed", weighted, dm, precision=HIGH)
    part = dw + jnp.einsum("ed,fdn->fen", w_bilinear, dm, precision=HIGH)
    part = part.astype(bf16).reshape(2 * size * width, tables, samples)
    part = jnp.moveaxis(part, 1, 0)
    parts = lax.all_to_all(part, "table", split_axis=0, concat_axis=0, tiled=True)

    pairs = jnp.stack(
        [
            jnp.concatenate(
                [x_lo[a][None] * y_lo[: a + 1], x_up[a][None] * y_up[a + 1 :]], axis=0
            )
            for a in range(size)
        ]
    )
    pairs = pairs.astype(bf16).reshape(size * size * width, cols)
    total = lax.dot_general(
        pairs, cotangent, (((1,), (1,)), ((), ())), preferred_element_type=f32
    )
    total = total.astype(bf16).reshape(subs, -1, hidden)
    total = lax.all_to_all(total, "sub", 0, 0, tiled=True)
    total = jnp.sum(total.astype(f32), axis=0) * (1.0 / total_samples)
    total = total.astype(bf16).reshape(-1, width, hidden)
    b_take = jnp.asarray(plan["b_take"])[me]
    arrived = []
    for c, perm in enumerate(plan["b_perms"]):
        piece = lax.dynamic_slice(total, (b_take[c], 0, 0), (1, width, hidden))[0]
        arrived.append(lax.ppermute(piece, BOTH, perm))
    rows_back = jnp.take(jnp.stack(arrived), jnp.asarray(plan["b_put"])[me], axis=0)
    rows_back = rows_back.reshape(-1, hidden)
    weight_grad = lax.dynamic_slice(
        rows_back, (jnp.asarray(plan["b_off"])[me], 0), (rows, hidden)
    ).astype(f32)

    collect = np.zeros((groups, 2 * tables), np.float32)
    for k, g in enumerate(needed):
        collect[g, k] = 1.0
    d_weighted = jnp.einsum(
        "gk,ken->gen",
        jnp.asarray(collect, bf16),
        parts.reshape(2 * tables, size * width, samples),
        preferred_element_type=f32,
    ).reshape(count, width, samples)
    own = jnp.einsum("ij,fjn->fin", signs, selected, preferred_element_type=f32) * scale
    _, back = jax.vjp(excited, own, w_squeeze, w_excite)
    field_grad, d_squeeze, d_excite = back(d_weighted)
    g_squeeze, g_excite, g_bilinear = lax.psum((d_squeeze, d_excite, d_bilinear), BOTH)
    slot_count = per_owner * tables
    onehot = (slot_index[None, :] == jnp.arange(slot_count, dtype=jnp.int32)[:, None]).astype(bf16)
    placed = jnp.einsum(
        "sf,fen->sen", onehot, field_grad.astype(bf16), preferred_element_type=f32
    ).astype(bf16)
    placed = placed.reshape(slot_count, 1, 1, width, samples)
    row_grads = lax.all_to_all(placed, "table", split_axis=0, concat_axis=1, tiled=True)
    inverse = 1.0 / total_samples
    return (row_grads, weight_grad, g_squeeze * inverse, g_excite * inverse, g_bilinear * inverse)


def solution(mesh):
    return jax.shard_map(
        on_device,
        mesh=mesh,
        in_specs=(
            P("table", None, "sub", None, None),
            P(),
            P(),
            P(),
            P(),
            P(BOTH, None),
            P(None, BOTH),
        ),
        out_specs=(P("table", None, "sub", None, None), P(BOTH, None), P(), P(), P()),
        check_vma=False,
    )
```

time: 596 us -> 561 us (0.941)
  blocking collectives: 145 us -> 68.3 us
  waiting for transfers between devices: 178 us -> 104 us
  starting transfers between devices: 51.3 us -> 125 us
  between operations: 16.9 us -> 54.9 us
  matrix products: 53.3 us -> 73.7 us
  local copies, waits for them, and re-layouts: 58 us -> 48.3 us
  other arithmetic: 85.3 us -> 77.7 us
    all_to_all x5 -> x4, waiting for transfers between devices: 151 us -> 5.6 us  [the longest x1 5.59 us: on_device(): total = lax.all_to_all(total, 'sub', 0, 0, tiled=True)]
    ppermute x0 -> x21, starting transfers between devices: none -> 83.4 us  [the longest x20 81.1 us: on_device(): arrived.append(lax.ppermute(piece, BOTH, perm))]
    psum x1, waiting for transfers between devices: 0.02 us -> 65.4 us  [on_device(): lax.psum((d_squeeze, d_excite, d_bilinear), BOTH)]
    unnamed x1 -> x0, blocking collectives: 58.7 us -> none
    reduce_sum x46 -> x1, other arithmetic: 58.9 us -> 2.4 us  [on_device(): total = jnp.sum(total.astype(f32), axis=0) * (1.0 / total_samples)]
    ppermute x0 -> x21, waiting for transfers between devices: none -> 33.2 us  [the longest x20 33.2 us: on_device(): arrived.append(lax.ppermute(piece, BOTH, perm))]
    all_gather x1, waiting for transfers between devices: 24.8 us -> 0.01 us  [on_device(): cotangent = lax.all_gather(tower_cotangent, 'table', axis=1, tiled=True)]
    unnamed x46 -> x14, other arithmetic: 2.52 us -> 23.5 us
  transfers between devices with their start and end apart: 10 -> 29, of which waited for: 6 -> 6; matrix products, arithmetic and copies ran while one was open for 33% -> 19% of each run, Pallas kernels for 0% -> 0%
where the time goes in v1:
time: 561 us; the launch traced here: 552 us
  starting transfers between devices  125 us (22%)
  waiting for transfers between devices  104 us (19%)
  other arithmetic  77.7 us (14%)
  matrix products  73.7 us (13%)
  blocking collectives  68.3 us (12%)
  between operations  54.9 us (10%)
  local copies, waits for them, and re-layouts  48.3 us (9%)
    ppermute x20, starting transfers between devices, on_device(): arrived.append(lax.ppermute(piece, BOTH, perm))  81.1 us
    psum x1, blocking collectives, on_device(): lax.psum((d_squeeze, d_excite, d_bilinear), BOTH)  68.3 us
    psum x1, waiting for transfers between devices, on_device(): lax.psum((d_squeeze, d_excite, d_bilinear), BOTH)  65.4 us
    ppermute x20, waiting for transfers between devices, on_device(): arrived.append(lax.ppermute(piece, BOTH, perm))  33.2 us
    unnamed x14, other arithmetic  23.5 us
    unnamed x145, local copies, waits for them, and re-layouts  17.4 us
    dot_general x1, matrix products, on_device(): lax.dot_general(pairs, cotangent, (((1,), (1,)), ((), ())), preferred_ele...  16.1 us
    dot_general x1, matrix products, on_device(): jnp.dot(weights, cotangent, preferred_element_type=f32).astype(bf16)  15.6 us
  transfers between devices with their start and end apart: 29, of which 6 were waited for; matrix products, arithmetic and copies ran while one was open for 19% of the time, Pallas kernels for 0%

profile of v1, /device:TPU:10, one launch (start us, length us, event | category | flops | bytes accessed | tf_op | source)
XLA Modules:
  0.0 551.6 jit_solution(5770102081123841496)
XLA Ops:
  9.7 8.4 %all-to-all-start.1 = ((bf16[3,32,1,32,128]{4,3,0,2,1:T(8,128)(2,1)}), bf16[3,32,1,32,128]{4,3,0,2,1:T(8,128)(2,1)S(1)}, u32[]{:S(2)}, u32[]{:S(2)}) async-start(bf16[3,32,1,32,128]{4,3,0,2,1:T(8,128)(2,1)} %copy.63), calls=%async_computation.1 | async-start | bytes 1572864 | tf_op jit(solution)/shard_map/all_to_all | solution.py:163
  18.2 1.5 slice.255
  19.7 2.3 collective-permute-start
  73.0 2.0 pad_maximum_fusion.3
  75.0 7.4 %all-to-all-start.2 = ((bf16[32,432,128]{2,1,0:T(8,128)(2,1)}), bf16[32,432,128]{2,1,0:T(8,128)(2,1)S(1)}, u32[]{:S(2)}, u32[]{:S(2)}) async-start(bf16[32,432,128]{2,1,0:T(8,128)(2,1)} %pad_maximum_fusion.3), calls=%async_computation.2 | async-start | bytes 7077888 | tf_op jit(solution)/shard_map/all_to_all | solution.py:174
  83.1 1.6 broadcast_select_fusion.3
  85.7 1.7 fusion.46
  87.3 3.1 collective-permute-start.1
  90.4 3.0 collective-permute-start.2
  93.4 6.4 %collective-permute-start.3 = (bf16[32,1024]{1,0:T(8,128)(2,1)S(1)}, bf16[32,1024]{1,0:T(8,128)(2,1)S(1)}, u32[]{:S(2)}, u32[]{:S(2)}) collective-permute-start(bf16[32,1024]{1,0:T(8,128)(2,1)S(1)} %get-tuple-element.72), channel_id=1, source_target_pairs={{0,112},{1,4},{2,8},{3,16},{4,20},{5,0},{6,5},{7,12},{8,13},{9,24}... | collective-permute-start | bytes 196616 | tf_op jit(solution)/shard_map/ppermute | solution.py:185
  99.8 6.0 %collective-permute-start.4 = (bf16[32,1024]{1,0:T(8,128)(2,1)S(1)}, bf16[32,1024]{1,0:T(8,128)(2,1)S(1)}, u32[]{:S(2)}, u32[]{:S(2)}) collective-permute-start(bf16[32,1024]{1,0:T(8,128)(2,1)S(1)} %get-tuple-element.73), channel_id=1, source_target_pairs={{0,0},{1,8},{2,12},{3,16},{4,24},{5,113},{6,4},{7,9},{8,17},{9,20}... | collective-permute-start | bytes 196616 | tf_op jit(solution)/shard_map/ppermute | solution.py:185
  105.8 4.1 collective-permute-start.5
  111.1 13.8 %collective-permute-done.1 = bf16[32,1024]{1,0:T(8,128)(2,1)S(1)} collective-permute-done((bf16[32,1024]{1,0:T(8,128)(2,1)S(1)}, bf16[32,1024]{1,0:T(8,128)(2,1)S(1)}, u32[]{:S(2)}, u32[]{:S(2)}) %collective-permute-start.1) | collective-permute-done | bytes 65568 | tf_op jit(solution)/shard_map/ppermute | solution.py:185
  124.9 5.0 collective-permute-start.6
  130.5 7.6 %collective-permute-start.7 = (bf16[32,1024]{1,0:T(8,128)(2,1)S(1)}, bf16[32,1024]{1,0:T(8,128)(2,1)S(1)}, u32[]{:S(2)}, u32[]{:S(2)}) collective-permute-start(bf16[32,1024]{1,0:T(8,128)(2,1)S(1)} %get-tuple-element.77), channel_id=1, source_target_pairs={{0,112},{1,4},{2,8},{3,16},{4,20},{5,0},{6,1},{7,12},{8,13},{9,24}... | collective-permute-start | bytes 196616 | tf_op jit(solution)/shard_map/ppermute | solution.py:185
  138.7 1.9 collective-permute-start.8
  141.3 8.9 %collective-permute-start.9 = (bf16[32,1024]{1,0:T(8,128)(2,1)S(1)}, bf16[32,1024]{1,0:T(8,128)(2,1)S(1)}, u32[]{:S(2)}, u32[]{:S(2)}) collective-permute-start(bf16[32,1024]{1,0:T(8,128)(2,1)S(1)} %get-tuple-element.69), channel_id=1, source_target_pairs={{0,0},{1,4},{2,8},{3,12},{4,20},{5,113},{6,1},{7,9},{8,16},{9,21},... | collective-permute-start | bytes 196616 | tf_op jit(solution)/shard_map/ppermute | solution.py:185
  154.0 2.5 gather_fusion
  156.5 2.0 bitcast_select_fusion
  158.6 2.8 broadcast_in_dim.88
  161.3 4.7 all-to-all-start
  166.4 3.7 copy.64
  170.1 5.8 %reshape.335 = bf16[12,32,4096]{2,1,0:T(8,128)(2,1)} reshape(bf16[384,32,128]{2,1,0:T(8,128)(2,1)} %copy.64) | data formatting | bytes 6291456 | tf_op jit(solution)/shard_map/reshape | solution.py:196
  176.5 6.2 %fusion.37 = f32[12,32,4096]{2,1,0:T(8,128)S(1)} fusion(f32[16,4096]{1,0:T(8,128)S(1)} %convolution_bitcast_fusion.1, f32[12,32,16]{1,0,2:T(8,128)} %broadcast_select_fusion.3), kind=kOutput, calls=%fused_computation.172 | convolution fusion | flops 302252032 | bytes 6578176 | tf_op jit(solution)/shard_map/dot_general | solution.py:203
  183.9 9.0 %convolution_bitcast_fusion = f32[12,32,4096]{2,1,0:T(8,128)} fusion(f32[12,32,4096]{2,1,0:T(8,128)S(1)} %bitcast_multiply_fusion, f32[32,32]{1,0:T(8,128)S(1)} %copy-done.20), kind=kOutput, calls=%fused_computation.9 | convolution fusion | flops 603979776 | bytes 12587008 | tf_op jit(solution)/shard_map/ed,fen->fdn/dot_general | solution.py:205
  192.9 7.0 %slice_select_fusion.1 = (f32[6,32,4096]{2,1,0:T(8,128)}, f32[6,32,4096]{2,1,0:T(8,128)S(1)}, f32[6,32,4096]{2,1,0:T(8,128)}) fusion(f32[12,32,4096]{2,1,0:T(8,128)} %convolution_bitcast_fusion, f32[12,32,4096]{2,1,0:T(8,128)S(1)} %bitcast_multiply_fusion, pred[]{:T(512)S(6)} %ge.31), kind=kLoop, calls=%fused_computation.16 | loop fusion | flops 2359296 | bytes 22020096 | tf_op jit(solution)/shard_map/jit(_where)/select_n | solution.py:207
  199.8 15.6 %convolution_convert_fusion = bf16[1152,4096]{1,0:T(8,128)(2,1)} fusion(bf16[1152,1024]{1,0:T(8,128)(2,1)} %bitcast.24, bf16[1024,4096]{1,0:T(8,128)(2,1)} %all-gather.2.cloned.1.call-done), kind=kOutput, calls=%fused_computation.4 | convolution fusion | flops 9668395008 | bytes 20185088 | tf_op jit(solution)/shard_map/dot_general | solution.py:193
  215.4 12.7 %convert.56 = f32[6,6,32,4096]{3,2,1,0:T(8,128)} convert(bf16[6,6,32,4096]{3,2,1,0:T(8,128)(2,1)} %bitcast.623) | non-fusion elementwise | flops 4718592 | bytes 28311552 | tf_op jit(solution)/shard_map/convert_element_type | solution.py:210
  228.1 2.2 multiply_dynamic-update-slice_fusion.3
  230.3 5.1 fusion.33
  235.4 5.2 add_dynamic-update-slice_fusion.2
  240.6 4.3 add_dynamic-update-slice_fusion.1
  247.4 1.4 add_dynamic-update-slice_fusion
  250.0 1.5 add_dynamic-update-slice_fusion.13
  251.5 1.5 multiply_dynamic-update-slice_fusion
  253.0 1.8 add_dynamic-update-slice_fusion.3
  254.8 1.5 multiply_dynamic-update-slice_fusion.1
  262.3 3.7 copy-done.19
  266.0 16.1 %convolution_convert_fusion.1 = bf16[1152,1024]{1,0:T(8,128)(2,1)} fusion(bf16[1152,4096]{1,0:T(8,128)(2,1)} %bitcast.698, bf16[1024,4096]{1,0:T(8,128)(2,1)} %all-gather.2.cloned.1.call-done), kind=kOutput, calls=%fused_computation.13 | convolution fusion | flops 9664856064 | bytes 20185088 | tf_op jit(solution)/shard_map/dot_general | solution.py:235
  282.1 4.5 all-to-all-start.5
  286.6 9.1 %select_add_fusion = (f32[6,32,4096]{2,1,0:T(8,128)S(1)}, f32[6,32,4096]{2,1,0:T(8,128)}, f32[6,32,4096]{2,1,0:T(8,128)S(1)}, f32[6,32,4096]{2,1,0:T(8,128)}) fusion(f32[6,32,4096]{2,1,0:T(8,128)} %broadcast_dynamic-update-slice_fusion, f32[6,32,4096]{2,1,0:T(8,128)} %fusion.35, pred[]{:T(512)S(6)} %ge.31, f32[6,32,4096]{2,1,0:T(8,128)} %get-tuple-element.45, ...), kind=kLoop, calls=%fused_computation.22 | loop fusion | flops 4718592 | bytes 25165824 | tf_op jit(solution)/shard_map/add | solution.py:216
  295.8 9.0 %fusion = bf16[12,32,4096]{2,1,0:T(8,128)(2,1)S(1)} fusion(f32[6,32,4096]{2,1,0:T(8,128)} %get-tuple-element.64, f32[6,32,4096]{2,1,0:T(8,128)} %get-tuple-element.66, f32[6,32,4096]{2,1,0:T(8,128)S(1)} %get-tuple-element.65, f32[6,32,4096]{2,1,0:T(8,128)S(1)} %get-tuple-element.63, f32[32,32]{1,0:T(8,128)S(1)} %copy-done.20), kind=kOutput, calls=%fused_computation.6 | convolution fusion | flops 610271232 | bytes 15732736 | tf_op jit(solution)/shard_map/ed,fdn->fen/dot_general | solution.py:221
  305.6 2.9 copy.95
  308.6 5.6 %all-to-all-done.5 = bf16[4,288,1024]{2,1,0:T(8,128)(2,1)} async-done(((bf16[4,288,1024]{2,1,0:T(8,128)(2,1)}), bf16[4,288,1024]{2,1,0:T(8,128)(2,1)}, u32[]{:S(2)}, u32[]{:S(2)}) %all-to-all-start.5) | async-done | bytes 2359328 | tf_op jit(solution)/shard_map/all_to_all | solution.py:239
  314.1 6.9 %all-to-all-start.3 = ((bf16[32,384,128]{2,1,0:T(8,128)(2,1)}), bf16[32,384,128]{2,1,0:T(8,128)(2,1)}, u32[]{:S(2)}, u32[]{:S(2)}) async-start(bf16[32,384,128]{2,1,0:T(8,128)(2,1)} %bitcast.620), calls=%async_computation.3 | async-start | bytes 6291456 | tf_op jit(solution)/shard_map/all_to_all | solution.py:224
  321.1 2.4 convert_reduce_fusion
  323.8 2.8 collective-permute-start.10
  326.6 7.8 %fusion.22 = f32[32,32]{1,0:T(8,128)S(1)} fusion(f32[12,32,4096]{2,1,0:T(8,128)} %copy-done.4, f32[6,32,4096]{2,1,0:T(8,128)S(1)} %copy-done.7, f32[6,32,4096]{2,1,0:T(8,128)S(1)} %get-tuple-element.63), kind=kOutput, calls=%fused_computation.70 | convolution fusion | flops 605552640 | bytes 12587008 | tf_op jit(solution)/shard_map/fen,fdn->ed/dot_general | solution.py:220
  334.4 2.1 collective-permute-start.11
  336.5 7.7 %collective-permute-start.12 = (bf16[32,1024]{1,0:T(8,128)(2,1)S(1)}, bf16[32,1024]{1,0:T(8,128)(2,1)S(1)}, u32[]{:S(2)}, u32[]{:S(2)}) collective-permute-start(bf16[32,1024]{1,0:T(8,128)(2,1)S(1)} %get-tuple-element.86), channel_id=1, source_target_pairs={{0,0},{4,1},{8,2},{16,3},{20,4},{112,5},{5,6},{12,7},{17,8},{24,9}... | collective-permute-start | bytes 196616 | tf_op jit(solution)/shard_map/ppermute | solution.py:246
  344.2 1.9 collective-permute-start.13
  346.1 3.1 collective-permute-start.14
  349.3 13.7 %collective-permute-done.10 = bf16[32,1024]{1,0:T(8,128)(2,1)S(1)} collective-permute-done((bf16[32,1024]{1,0:T(8,128)(2,1)S(1)}, bf16[32,1024]{1,0:T(8,128)(2,1)S(1)}, u32[]{:S(2)}, u32[]{:S(2)}) %collective-permute-start.10) | collective-permute-done | bytes 65568 | tf_op jit(solution)/shard_map/ppermute | solution.py:246
  362.9 1.9 collective-permute-start.15
  364.9 1.7 collective-permute-done.11
  366.5 1.9 collective-permute-start.16
  368.5 6.2 %collective-permute-start.17 = (bf16[32,1024]{1,0:T(8,128)(2,1)S(1)}, bf16[32,1024]{1,0:T(8,128)(2,1)S(1)}, u32[]{:S(2)}, u32[]{:S(2)}) collective-permute-start(bf16[32,1024]{1,0:T(8,128)(2,1)S(1)} %get-tuple-element.81), channel_id=1, source_target_pairs={{112,0},{4,1},{8,2},{12,3},{24,4},{0,5},{1,6},{9,7},{16,8},{20,9},... | collective-permute-start | bytes 196616 | tf_op jit(solution)/shard_map/ppermute | solution.py:246
  374.7 5.6 %collective-permute-start.18 = (bf16[32,1024]{1,0:T(8,128)(2,1)S(1)}, bf16[32,1024]{1,0:T(8,128)(2,1)S(1)}, u32[]{:S(2)}, u32[]{:S(2)}) collective-permute-start(bf16[32,1024]{1,0:T(8,128)(2,1)S(1)} %get-tuple-element.80), channel_id=1, source_target_pairs={{112,0},{0,1},{8,2},{12,3},{20,4},{24,5},{9,7},{17,9},{1,11},{5,12... | collective-permute-start | bytes 196616 | tf_op jit(solution)/shard_map/ppermute | solution.py:246
  382.4 4.1 collective-permute-done.19
  388.3 3.7 fusion.2
  398.0 9.1 %all-to-all-start.4 = ((bf16[96,1,1,32,128]{4,3,2,1,0:T(8,128)(2,1)}), bf16[96,1,1,32,128]{4,3,2,1,0:T(8,128)(2,1)S(1)}, u32[]{:S(2)}, u32[]{:S(2)}) async-start(bf16[96,1,1,32,128]{4,3,2,1,0:T(8,128)(2,1)} %copy.75), calls=%async_computation.4 | async-start | bytes 1572864 | tf_op jit(solution)/shard_map/all_to_all | solution.py:272
  407.2 68.3 %all-reduce = (f32[16,48]{1,0:T(8,128)S(1)}, f32[32,32]{1,0:T(8,128)S(1)}) all-reduce(f32[16,48]{1,0:T(8,128)S(1)} %fusion.58, f32[32,32]{1,0:T(8,128)S(1)} %fusion.22), channel_id=1, replica_groups=mesh['table'=32,'sub'=4] {'table','sub'}, use_global_device_ids=true, to_apply=%region_3.4 | all-reduce | flops 1792 | bytes 14336 | tf_op jit(solution)/shard_map/psum | solution.py:265
  476.6 65.4 %all-reduce.3.cloned.1.call-done = f32[1536,16]{0,1:T(8,128)} async-done(((f32[1536,16]{0,1:T(8,128)}), f32[1536,16]{0,1:T(8,128)}) %all-reduce.3.cloned.1.call-update) | async-done | bytes 98320 | tf_op jit(solution)/shard_map/psum | solution.py:265
  542.1 1.5 broadcast_multiply_fusion
  (252 shorter events, 46.9 us)
Async XLA Ops:
  7.2 1.2 copy-start
  7.2 46.9 %copy-start.27 = (s32[128]{0:T(128)S(1)}, s32[128]{0:T(128)}, u32[]{:S(2)}) copy-start(s32[128]{0:T(128)} %constant.135.clone) | copy-start | bytes 1540
  7.2 42.7 %copy-start.17 = (f32[1536,16]{0,1:T(8,128)S(1)}, f32[1536,16]{0,1:T(8,128)}, u32[]{:S(2)}) copy-start(f32[1536,16]{0,1:T(8,128)} %param.17) | copy-start | bytes 294916
  7.2 42.8 %copy-start.26 = (s32[48]{0:T(128)S(1)}, s32[48]{0:T(128)}, u32[]{:S(2)}) copy-start(s32[48]{0:T(128)} %param.15) | copy-start | bytes 580
  9.7 61.3 %all-to-all-start.1 = ((bf16[3,32,1,32,128]{4,3,0,2,1:T(8,128)(2,1)}), bf16[3,32,1,32,128]{4,3,0,2,1:T(8,128)(2,1)S(1)}, u32[]{:S(2)}, u32[]{:S(2)}) async-start(bf16[3,32,1,32,128]{4,3,0,2,1:T(8,128)(2,1)} %copy.63), calls=%async_computation.1 | async-start | bytes 1572864 | tf_op jit(solution)/shard_map/all_to_all | solution.py:163
  18.1 181.7 %all-gather.2.cloned.1.call-start = ((), (), s32[]{:S(2)}) async-start(), calls=%async_computation.6 | async-start | bytes 8650752 | tf_op jit(solution)/shard_map/all_gather | solution.py:192
  19.7 66.0 %collective-permute-start = (bf16[32,1024]{1,0:T(8,128)(2,1)}, bf16[32,1024]{1,0:T(8,128)(2,1)}, u32[]{:S(2)}, u32[]{:S(2)}) collective-permute-start(bf16[32,1024]{1,0:T(8,128)(2,1)} %slice.255), channel_id=1, source_target_pairs={{1,0},{2,1},{3,2},{4,3},{5,4},{6,5},{7,6},{8,7},{9,8},{10,9},{11,1... | collective-permute-start | bytes 196616 | tf_op jit(solution)/shard_map/ppermute | solution.py:177
  50.2 0.7 copy-start.23
  71.7 1.0 copy-start.9
  75.0 83.5 %all-to-all-start.2 = ((bf16[32,432,128]{2,1,0:T(8,128)(2,1)}), bf16[32,432,128]{2,1,0:T(8,128)(2,1)S(1)}, u32[]{:S(2)}, u32[]{:S(2)}) async-start(bf16[32,432,128]{2,1,0:T(8,128)(2,1)} %pad_maximum_fusion.3), calls=%async_computation.2 | async-start | bytes 7077888 | tf_op jit(solution)/shard_map/all_to_all | solution.py:174
  87.3 37.5 %collective-permute-start.1 = (bf16[32,1024]{1,0:T(8,128)(2,1)S(1)}, bf16[32,1024]{1,0:T(8,128)(2,1)S(1)}, u32[]{:S(2)}, u32[]{:S(2)}) collective-permute-start(bf16[32,1024]{1,0:T(8,128)(2,1)S(1)} %get-tuple-element.70), channel_id=1, source_target_pairs={{0,0},{1,4},{2,12},{3,20},{4,24},{5,112},{6,1},{7,8},{8,16},{9,21}... | collective-permute-start | bytes 196616 | tf_op jit(solution)/shard_map/ppermute | solution.py:185
  90.4 40.0 %collective-permute-start.2 = (bf16[32,1024]{1,0:T(8,128)(2,1)S(1)}, bf16[32,1024]{1,0:T(8,128)(2,1)S(1)}, u32[]{:S(2)}, u32[]{:S(2)}) collective-permute-start(bf16[32,1024]{1,0:T(8,128)(2,1)S(1)} %get-tuple-element.71), channel_id=1, source_target_pairs={{0,112},{1,0},{2,8},{3,16},{4,20},{5,24},{6,4},{7,9},{8,12},{9,21}... | collective-permute-start | bytes 196616 | tf_op jit(solution)/shard_map/ppermute | solution.py:185
  93.4 45.3 %collective-permute-start.3 = (bf16[32,1024]{1,0:T(8,128)(2,1)S(1)}, bf16[32,1024]{1,0:T(8,128)(2,1)S(1)}, u32[]{:S(2)}, u32[]{:S(2)}) collective-permute-start(bf16[32,1024]{1,0:T(8,128)(2,1)S(1)} %get-tuple-element.72), channel_id=1, source_target_pairs={{0,112},{1,4},{2,8},{3,16},{4,20},{5,0},{6,5},{7,12},{8,13},{9,24}... | collective-permute-start | bytes 196616 | tf_op jit(solution)/shard_map/ppermute | solution.py:185
  99.8 41.5 %collective-permute-start.4 = (bf16[32,1024]{1,0:T(8,128)(2,1)S(1)}, bf16[32,1024]{1,0:T(8,128)(2,1)S(1)}, u32[]{:S(2)}, u32[]{:S(2)}) collective-permute-start(bf16[32,1024]{1,0:T(8,128)(2,1)S(1)} %get-tuple-element.73), channel_id=1, source_target_pairs={{0,0},{1,8},{2,12},{3,16},{4,24},{5,113},{6,4},{7,9},{8,17},{9,20}... | collective-permute-start | bytes 196616 | tf_op jit(solution)/shard_map/ppermute | solution.py:185
  105.8 45.1 %collective-permute-start.5 = (bf16[32,1024]{1,0:T(8,128)(2,1)S(1)}, bf16[32,1024]{1,0:T(8,128)(2,1)S(1)}, u32[]{:S(2)}, u32[]{:S(2)}) collective-permute-start(bf16[32,1024]{1,0:T(8,128)(2,1)S(1)} %get-tuple-element.74), channel_id=1, source_target_pairs={{0,0},{1,4},{2,12},{3,16},{4,24},{5,113},{6,5},{7,8},{8,17},{9,20}... | collective-permute-start | bytes 196616 | tf_op jit(solution)/shard_map/ppermute | solution.py:185
  124.9 26.6 %collective-permute-start.6 = (bf16[32,1024]{1,0:T(8,128)(2,1)S(1)}, bf16[32,1024]{1,0:T(8,128)(2,1)S(1)}, u32[]{:S(2)}, u32[]{:S(2)}) collective-permute-start(bf16[32,1024]{1,0:T(8,128)(2,1)S(1)} %get-tuple-element.76), channel_id=1, source_target_pairs={{0,112},{1,4},{2,12},{3,16},{4,24},{6,0},{7,8},{8,13},{9,20},{10,1... | collective-permute-start | bytes 196616 | tf_op jit(solution)/shard_map/ppermute | solution.py:185
  130.5 21.7 %collective-permute-start.7 = (bf16[32,1024]{1,0:T(8,128)(2,1)S(1)}, bf16[32,1024]{1,0:T(8,128)(2,1)S(1)}, u32[]{:S(2)}, u32[]{:S(2)}) collective-permute-start(bf16[32,1024]{1,0:T(8,128)(2,1)S(1)} %get-tuple-element.77), channel_id=1, source_target_pairs={{0,112},{1,4},{2,8},{3,16},{4,20},{5,0},{6,1},{7,12},{8,13},{9,24}... | collective-permute-start | bytes 196616 | tf_op jit(solution)/shard_map/ppermute | solution.py:185
  138.7 14.1 %collective-permute-start.8 = (bf16[32,1024]{1,0:T(8,128)(2,1)S(1)}, bf16[32,1024]{1,0:T(8,128)(2,1)S(1)}, u32[]{:S(2)}, u32[]{:S(2)}) collective-permute-start(bf16[32,1024]{1,0:T(8,128)(2,1)S(1)} %get-tuple-element.75), channel_id=1, source_target_pairs={{0,112},{1,0},{2,8},{3,12},{4,20},{5,24},{6,4},{7,5},{8,16},{9,17}... | collective-permute-start | bytes 196616 | tf_op jit(solution)/shard_map/ppermute | solution.py:185
  141.3 12.1 %collective-permute-start.9 = (bf16[32,1024]{1,0:T(8,128)(2,1)S(1)}, bf16[32,1024]{1,0:T(8,128)(2,1)S(1)}, u32[]{:S(2)}, u32[]{:S(2)}) collective-permute-start(bf16[32,1024]{1,0:T(8,128)(2,1)S(1)} %get-tuple-element.69), channel_id=1, source_target_pairs={{0,0},{1,4},{2,8},{3,12},{4,20},{5,113},{6,1},{7,9},{8,16},{9,21},... | collective-permute-start | bytes 196616 | tf_op jit(solution)/shard_map/ppermute | solution.py:185
  161.3 38.5 %all-to-all-start = ((bf16[4,288,1024]{2,1,0:T(8,128)(2,1)}), bf16[4,288,1024]{2,1,0:T(8,128)(2,1)}, u32[]{:S(2)}, u32[]{:S(2)}) async-start(bf16[4,288,1024]{2,1,0:T(8,128)(2,1)} %broadcast_in_dim.88), calls=%async_computation | async-start | bytes 4718592 | tf_op jit(solution)/shard_map/all_to_all | solution.py:188
  170.1 5.8 %copy-start.21 = (f32[16,48]{1,0:T(8,128)S(1)}, f32[16,48]{1,0:T(8,128)}, u32[]{:S(2)}) copy-start(f32[16,48]{1,0:T(8,128)} %param.16) | copy-start | bytes 9220
  176.5 6.2 %copy-start.8 = (bf16[12,32,4096]{2,1,0:T(8,128)(2,1)S(1)}, bf16[12,32,4096]{2,1,0:T(8,128)(2,1)}, u32[]{:S(2)}) copy-start(bf16[12,32,4096]{2,1,0:T(8,128)(2,1)} %reshape.335) | copy-start | bytes 9437188
  182.7 1.2 copy-start.20
  183.8 9.0 %copy-start.4 = (f32[12,32,4096]{2,1,0:T(8,128)}, f32[12,32,4096]{2,1,0:T(8,128)S(1)}, u32[]{:S(2)}) copy-start(f32[12,32,4096]{2,1,0:T(8,128)S(1)} %bitcast_multiply_fusion) | copy-start | bytes 18874372
  228.1 12.5 %copy-start.2 = (f32[6,6,32,4096]{3,2,1,0:T(8,128)S(1)}, f32[6,6,32,4096]{3,2,1,0:T(8,128)}, u32[]{:S(2)}) copy-start(f32[6,6,32,4096]{3,2,1,0:T(8,128)} %convert.56) | copy-start | bytes 56623108
  240.6 4.3 copy-start.5
  244.9 2.5 copy-start.3
  244.9 3.9 slice-start
  247.4 2.6 slice-start.1
  258.5 1.0 copy-start.16
  258.7 1.1 copy-start.14
  258.9 1.1 copy-start.15
  259.6 1.1 copy-start.13
  260.0 1.1 copy-start.12
  260.2 1.1 copy-start.11
  262.3 3.7 copy-start.19
  282.1 32.0 %all-to-all-start.5 = ((bf16[4,288,1024]{2,1,0:T(8,128)(2,1)}), bf16[4,288,1024]{2,1,0:T(8,128)(2,1)}, u32[]{:S(2)}, u32[]{:S(2)}) async-start(bf16[4,288,1024]{2,1,0:T(8,128)(2,1)} %bitcast.124), calls=%async_computation.5 | async-start | bytes 4718592 | tf_op jit(solution)/shard_map/all_to_all | solution.py:239
  295.8 9.1 %copy-start.6 = (f32[6,32,4096]{2,1,0:T(8,128)}, f32[6,32,4096]{2,1,0:T(8,128)S(1)}, u32[]{:S(2)}) copy-start(f32[6,32,4096]{2,1,0:T(8,128)S(1)} %get-tuple-element.65) | copy-start | bytes 9437188
  314.1 74.2 %all-to-all-start.3 = ((bf16[32,384,128]{2,1,0:T(8,128)(2,1)}), bf16[32,384,128]{2,1,0:T(8,128)(2,1)}, u32[]{:S(2)}, u32[]{:S(2)}) async-start(bf16[32,384,128]{2,1,0:T(8,128)(2,1)} %bitcast.620), calls=%async_computation.3 | async-start | bytes 6291456 | tf_op jit(solution)/shard_map/all_to_all | solution.py:224
  321.1 221.0 %all-reduce.3.cloned.1.call-start = ((), (), s32[]{:S(2)}) async-start(), calls=%async_computation.7 | async-start | bytes 196608 | tf_op jit(solution)/shard_map/psum | solution.py:265
  321.1 5.4 copy-start.7
  323.7 63.4 %copy-start.25 = (pred[282]{0:T(512)(128)(4,1)S(1)}, pred[282]{0:T(512)(128)(4,1)}, u32[]{:S(2)}) copy-start(pred[282]{0:T(512)(128)(4,1)} %dynamic-slice) | copy-start | bytes 850
  323.8 39.2 %collective-permute-start.10 = (bf16[32,1024]{1,0:T(8,128)(2,1)S(1)}, bf16[32,1024]{1,0:T(8,128)(2,1)S(1)}, u32[]{:S(2)}, u32[]{:S(2)}) collective-permute-start(bf16[32,1024]{1,0:T(8,128)(2,1)S(1)} %get-tuple-element.88), channel_id=1, source_target_pairs={{0,0},{4,1},{12,2},{16,3},{24,4},{113,5},{5,6},{8,7},{13,8},{20,9}... | collective-permute-start | bytes 196616 | tf_op jit(solution)/shard_map/ppermute | solution.py:246
  334.4 53.9 %copy-start.22 = (bf16[8,64,1]{1,0,2:T(8,128)(2,1)S(1)}, bf16[8,64,1]{1,0,2:T(8,128)(2,1)}, u32[]{:S(2)}) copy-start(bf16[8,64,1]{1,0,2:T(8,128)(2,1)} %constant.139) | copy-start | bytes 3076
  334.4 32.1 %collective-permute-start.11 = (bf16[32,1024]{1,0:T(8,128)(2,1)S(1)}, bf16[32,1024]{1,0:T(8,128)(2,1)S(1)}, u32[]{:S(2)}, u32[]{:S(2)}) collective-permute-start(bf16[32,1024]{1,0:T(8,128)(2,1)S(1)} %get-tuple-element.87), channel_id=1, source_target_pairs={{0,0},{4,1},{12,2},{16,3},{20,4},{24,5},{1,6},{8,7},{13,8},{21,9},... | collective-permute-start | bytes 196616 | tf_op jit(solution)/shard_map/ppermute | solution.py:246
  336.5 32.0 %collective-permute-start.12 = (bf16[32,1024]{1,0:T(8,128)(2,1)S(1)}, bf16[32,1024]{1,0:T(8,128)(2,1)S(1)}, u32[]{:S(2)}, u32[]{:S(2)}) collective-permute-start(bf16[32,1024]{1,0:T(8,128)(2,1)S(1)} %get-tuple-element.86), channel_id=1, source_target_pairs={{0,0},{4,1},{8,2},{16,3},{20,4},{112,5},{5,6},{12,7},{17,8},{24,9}... | collective-permute-start | bytes 196616 | tf_op jit(solution)/shard_map/ppermute | solution.py:246
  344.2 30.5 %collective-permute-start.13 = (bf16[32,1024]{1,0:T(8,128)(2,1)S(1)}, bf16[32,1024]{1,0:T(8,128)(2,1)S(1)}, u32[]{:S(2)}, u32[]{:S(2)}) collective-permute-start(bf16[32,1024]{1,0:T(8,128)(2,1)S(1)} %get-tuple-element.85), channel_id=1, source_target_pairs={{112,0},{0,1},{8,2},{12,3},{20,4},{24,5},{4,6},{9,7},{16,8},{21,9}... | collective-permute-start | bytes 196616 | tf_op jit(solution)/shard_map/ppermute | solution.py:246
  346.1 34.2 %collective-permute-start.14 = (bf16[32,1024]{1,0:T(8,128)(2,1)S(1)}, bf16[32,1024]{1,0:T(8,128)(2,1)S(1)}, u32[]{:S(2)}, u32[]{:S(2)}) collective-permute-start(bf16[32,1024]{1,0:T(8,128)(2,1)S(1)} %get-tuple-element.84), channel_id=1, source_target_pairs={{112,0},{8,1},{12,2},{16,3},{20,4},{0,5},{4,6},{5,7},{13,8},{24,9}... | collective-permute-start | bytes 196616 | tf_op jit(solution)/shard_map/ppermute | solution.py:246
  362.9 18.7 %collective-permute-start.15 = (bf16[32,1024]{1,0:T(8,128)(2,1)S(1)}, bf16[32,1024]{1,0:T(8,128)(2,1)S(1)}, u32[]{:S(2)}, u32[]{:S(2)}) collective-permute-start(bf16[32,1024]{1,0:T(8,128)(2,1)S(1)} %get-tuple-element.83), channel_id=1, source_target_pairs={{0,0},{4,1},{8,2},{20,3},{24,4},{113,5},{1,6},{12,7},{16,8},{21,9}... | collective-permute-start | bytes 196616 | tf_op jit(solution)/shard_map/ppermute | solution.py:246
  366.5 15.8 %collective-permute-start.16 = (bf16[32,1024]{1,0:T(8,128)(2,1)S(1)}, bf16[32,1024]{1,0:T(8,128)(2,1)S(1)}, u32[]{:S(2)}, u32[]{:S(2)}) collective-permute-start(bf16[32,1024]{1,0:T(8,128)(2,1)S(1)} %get-tuple-element.82), channel_id=1, source_target_pairs={{112,0},{0,1},{12,2},{16,3},{24,4},{113,5},{4,6},{8,7},{17,8},{20,... | collective-permute-start | bytes 196616 | tf_op jit(solution)/shard_map/ppermute | solution.py:246
  368.5 13.9 %collective-permute-start.17 = (bf16[32,1024]{1,0:T(8,128)(2,1)S(1)}, bf16[32,1024]{1,0:T(8,128)(2,1)S(1)}, u32[]{:S(2)}, u32[]{:S(2)}) collective-permute-start(bf16[32,1024]{1,0:T(8,128)(2,1)S(1)} %get-tuple-element.81), channel_id=1, source_target_pairs={{112,0},{4,1},{8,2},{12,3},{24,4},{0,5},{1,6},{9,7},{16,8},{20,9},... | collective-permute-start | bytes 196616 | tf_op jit(solution)/shard_map/ppermute | solution.py:246
  374.7 7.7 %collective-permute-start.18 = (bf16[32,1024]{1,0:T(8,128)(2,1)S(1)}, bf16[32,1024]{1,0:T(8,128)(2,1)S(1)}, u32[]{:S(2)}, u32[]{:S(2)}) collective-permute-start(bf16[32,1024]{1,0:T(8,128)(2,1)S(1)} %get-tuple-element.80), channel_id=1, source_target_pairs={{112,0},{0,1},{8,2},{12,3},{20,4},{24,5},{9,7},{17,9},{1,11},{5,12... | collective-permute-start | bytes 196616 | tf_op jit(solution)/shard_map/ppermute | solution.py:246
  380.3 6.2 %collective-permute-start.19 = (bf16[32,1024]{1,0:T(8,128)(2,1)S(1)}, bf16[32,1024]{1,0:T(8,128)(2,1)S(1)}, u32[]{:S(2)}, u32[]{:S(2)}) collective-permute-start(bf16[32,1024]{1,0:T(8,128)(2,1)S(1)} %get-tuple-element.79), channel_id=1, source_target_pairs={{4,1},{8,2},{16,3},{20,4},{0,6},{5,7},{12,8},{17,9},{24,10},{1,11}... | collective-permute-start | bytes 196616 | tf_op jit(solution)/shard_map/ppermute | solution.py:246
  381.6 4.8 collective-permute-start.20
  388.3 3.9 copy-start.10
  392.0 2.0 copy-start.18
  392.6 3.7 copy-start.24
  396.1 148.4 %copy-start.1 = (bf16[3,32,1,32,128]{4,3,2,1,0:T(8,128)(2,1)S(1)}, bf16[3,32,1,32,128]{4,3,2,1,0:T(8,128)(2,1)}, u32[]{:S(2)}) copy-start(bf16[3,32,1,32,128]{4,3,2,1,0:T(8,128)(2,1)} %param.14) | copy-start | bytes 2359300
  398.0 145.6 %all-to-all-start.4 = ((bf16[96,1,1,32,128]{4,3,2,1,0:T(8,128)(2,1)}), bf16[96,1,1,32,128]{4,3,2,1,0:T(8,128)(2,1)S(1)}, u32[]{:S(2)}, u32[]{:S(2)}) async-start(bf16[96,1,1,32,128]{4,3,2,1,0:T(8,128)(2,1)} %copy.75), calls=%async_computation.4 | async-start | bytes 1572864 | tf_op jit(solution)/shard_map/all_to_all | solution.py:272
Sparse Core Ops, SparseCore 0:
  22.2 59.9 all-gather.1
  396.0 146.0 all-reduce.2
